TPU v7x, 8 devices: a whole 2x2x1 slice. The times are simulated.
8 devices in a mesh: dp: 2 (over z, y), cp: 4 (over x, core).
Axes of the slice: x: 2, y: 2, z: 1, core: 2. Of those that a mesh axis runs over, the one named last changes fastest.
Arguments:
- latent: bfloat16 [16, 4, 128, 512], P(('dp', 'cp')), parts along dimension 0
- conv_w: bfloat16 [4, 3, 3, 3, 512, 512], replicated
- conv_b: float32 [4, 512], replicated
- norm_in_scale: float32 [2, 512], replicated
- norm_in_shift: float32 [2, 512], replicated
- norm_mid_scale: float32 [2, 16, 512], P(None, ('dp', 'cp')), parts along dimension 1
- norm_mid_shift: float32 [2, 16, 512], P(None, ('dp', 'cp')), parts along dimension 1
Outputs:
- output: bfloat16 [16, 4, 128, 512], P(('dp', 'cp')), parts along dimension 0
There are 2 independent parts. A program takes and returns all parts, laid end to end along the dimension named above; an argument that names none is the same for every part.
All inputs are finite; a program needn't handle non-finite values.
Results may differ from a plain program's by a relative error of at most 0.0134452.
Values are sent between devices in bfloat16 or wider.
A program may use at most 1 GiB of HBM per device.

v0:
```python
import functools

import jax
import jax.numpy as jnp
from jax import lax
from jax.experimental import pallas as pl
from jax.experimental.pallas import tpu as pltpu
from jax.sharding import PartitionSpec as P

NUM_GROUPS = 32
EPSILON = 1e-6
EXPLICIT = False
MESH = pl.DeviceIdType.MESH
F32 = jnp.float32
BF16 = jnp.bfloat16

N_CONV = 4
N_FR = 2
N_ROW = 4
N_COL = 128
N_CH = 512
TILE = 16
N_TILE = N_COL // TILE
PAD_COL = N_COL + 2 * TILE
HALF = 256


def kernel(
    cp_size,
    x_hbm, w_hbm, bias_ref, in_scale, in_shift, mid_scale, mid_shift,
    out_hbm,
    x_in, raw, halo, act, wts, part, tx, rx, gains, shifts, h_scale, h_shift, mean_ref, rstd_ref, tmp,
    x_sem, w_sem, st_send, st_recv, h_send, h_recv, p_send, p_recv, o_sem,
    *extra,
):
    if EXPLICIT:
        pl.run_scoped(
            functools.partial(
                body, cp_size, x_hbm, w_hbm, bias_ref, in_scale, in_shift, mid_scale, mid_shift, out_hbm,
                x_in, raw, halo, act, wts, part, tx, rx, gains, shifts, h_scale, h_shift, mean_ref, rstd_ref, tmp,
                x_sem, w_sem, st_send, st_recv, h_send, h_recv, p_send, p_recv, o_sem,
            ),
            *[pltpu.ACC(m)((N_COL, HALF), F32) for m in range(2) for _ in range(N_FR * N_ROW)],
        )
    else:
        body(
            cp_size, x_hbm, w_hbm, bias_ref, in_scale, in_shift, mid_scale, mid_shift, out_hbm,
            x_in, raw, halo, act, wts, part, tx, rx, gains, shifts, h_scale, h_shift, mean_ref, rstd_ref, tmp,
            x_sem, w_sem, st_send, st_recv, h_send, h_recv, p_send, p_recv, o_sem, *extra,
        )


def body(
    cp_size, x_hbm, w_hbm, bias_ref, in_scale, in_shift, mid_scale, mid_shift, out_hbm,
    x_in, raw, halo, act, wts, part, tx, rx, gains, shifts, h_scale, h_shift, mean_ref, rstd_ref, tmp,
    x_sem, w_sem, st_send, st_recv, h_send, h_recv, p_send, p_recv, o_sem,
    *accs,
):
    cp = lax.axis_index("cp")
    count = float(N_FR * cp_size * N_ROW * N_COL * (N_CH // NUM_GROUPS))
    first, last = cp == 0, cp == cp_size - 1
    peers = [lax.rem(cp + d, cp_size) for d in range(1, cp_size)]
    right = lax.rem(cp + 1, cp_size)

    def acc_of(m, t, p):
        return accs[(m * N_FR + t) * N_ROW + p]

    def mm_push(slot, k, dp, dq, kt, m, reg):
        off = ((dp + 1) * 3 + dq + 1) * N_CH + kt * HALF
        w = wts[slot, k, off : off + HALF, m * HALF : (m + 1) * HALF]
        pltpu.matmul_push_rhs(w, staging_register=reg, mxu_index=m)

    def mm_step(slot, t, k, dp, dq, kt, rows, reg):
        rows = [p for p in rows if 0 <= p + dp < N_ROW]
        if EXPLICIT:
            for m in range(2):
                mm_push(slot, k, dp, dq, kt, m, reg)
        for i, p in enumerate(rows):
            lhs = act[t + k, p + dp, TILE * (1 + dq) : TILE * (1 + dq) + N_COL, kt * HALF : (kt + 1) * HALF]
            for m in range(2):
                if EXPLICIT:
                    pltpu.matmul_acc_lhs(acc_of(m, t, p), lhs, load_staged_rhs=reg if i == 0 else None)
                else:
                    off = ((dp + 1) * 3 + dq + 1) * N_CH + kt * HALF
                    w = wts[slot, k, off : off + HALF, m * HALF : (m + 1) * HALF]
                    accs[0][t, p, m] += jnp.dot(lhs, w, preferred_element_type=F32)

    def pop(m, t, p):
        if EXPLICIT:
            return pltpu.matmul_pop(acc_of(m, t, p))
        val = accs[0][t, p, m]
        accs[0][t, p, m] = jnp.zeros((N_COL, HALF), F32)
        return val

    def steps_of(t, k, kts=(0, 1), rows=range(N_ROW)):
        return [(t, k, dp, dq, kt, tuple(rows)) for kt in kts for dp in (0, -1, 1) for dq in (0, -1, 1)]

    def run(slot, steps, thunks=(), upto=1.0):
        done, span = 0, max(1, int(len(steps) * upto))
        for i, (t, k, dp, dq, kt, rows) in enumerate(steps):
            mm_step(slot, t, k, dp, dq, kt, rows, i % 2)
            want = min(len(thunks), -(-len(thunks) * (i + 1) // span))
            for thunk in thunks[done:want]:
                thunk()
            done = want

    def add_moments(val, half):
        cut = slice(half * HALF, (half + 1) * HALF)
        rows = val.reshape(N_COL // 8, 8, HALF)
        part[0, :, cut] += jnp.sum(rows, axis=0)
        part[1, :, cut] += jnp.sum(rows * rows, axis=0)

    def norm(read, c, f, p, half):
        cut = slice(half * HALF, (half + 1) * HALF)
        gain = rstd_ref[0:1, cut] * gains[c, f : f + 1, cut]
        val = (read(p, cut).astype(F32) - mean_ref[0:1, cut]) * gain + shifts[c, f : f + 1, cut]
        val = 0.5 * val.astype(BF16).astype(F32)
        val = val + val * jnp.tanh(val)
        act[f, p, TILE : TILE + N_COL, cut] = val.astype(BF16)
        row = lax.broadcasted_iota(jnp.int32, (TILE, HALF), 0)
        low = jnp.where(row == 0, 0.0, pltpu.roll(val[N_COL - TILE :], 1, 0))
        act[f, p, 0:TILE, cut] = low.astype(BF16)
        high = jnp.where(row == TILE - 1, 0.0, pltpu.roll(val[:TILE], TILE - 1, 0))
        act[f, p, TILE + N_COL :, cut] = high.astype(BF16)

    def epilogue(c, par, t, p, m):
        cut = slice(m * HALF, (m + 1) * HALF)
        flag = par.astype(F32)
        conv = (pop(m, t, p) + bias_ref[pl.ds(c, 1), cut]).astype(BF16).astype(F32)
        val = (raw[0, t, p, :, cut].astype(F32) * flag + conv).astype(BF16)
        raw[1 - par, t, p, :, cut] = val
        add_moments(val.astype(F32), m)

    def finish_moments(slot):
        for i in range(2):
            total = jnp.sum(part[i], axis=0, keepdims=True)
            for j in range(4):
                tx[slot, 4 * i + j : 4 * i + j + 1, :] = total[:, j * 128 : (j + 1) * 128]
        part[...] = jnp.zeros_like(part)

    def statistics(slot):
        total = tx[slot]
        for d in range(cp_size - 1):
            total = total + rx[slot, d]
        lane = lax.broadcasted_iota(jnp.int32, total.shape, 1)
        for shift in (1, 2, 4, 8):
            total = total + jnp.where(
                (lane & shift) == 0, pltpu.roll(total, 128 - shift, 1), pltpu.roll(total, shift, 1)
            )
        mean = total[0:4] / count
        var = total[4:8] / count - mean * mean
        rstd = lax.rsqrt(var + EPSILON)
        for j in range(4):
            mean_ref[0:1, j * 128 : (j + 1) * 128] = mean[j : j + 1]
            rstd_ref[0:1, j * 128 : (j + 1) * 128] = rstd[j : j + 1]

    def w_copy(c, k):
        slot = lax.rem(c, 2)
        return pltpu.make_async_copy(w_hbm.at[c, k], wts.at[slot, k], w_sem.at[slot, k])

    def st_copy(slot, d):
        return pltpu.make_async_remote_copy(
            src_ref=tx.at[slot], dst_ref=rx.at[slot, d], send_sem=st_send.at[slot, d], recv_sem=st_recv.at[slot, d],
            device_id={"cp": peers[d]}, device_id_type=MESH,
        )

    def halo_copy(par, hs, t):
        return pltpu.make_async_remote_copy(
            src_ref=raw.at[par, t], dst_ref=halo.at[hs, t], send_sem=h_send.at[t], recv_sem=h_recv.at[hs, t],
            device_id={"cp": right}, device_id_type=MESH,
        )

    def own_copy(par, hs, t):
        return pltpu.make_async_copy(raw.at[par, 0], halo.at[hs, t], h_recv.at[hs, t])

    def param_copy(i):
        src, dst = ((mid_scale, h_scale), (mid_shift, h_shift))[i]
        return pltpu.make_async_remote_copy(
            src_ref=src, dst_ref=dst, send_sem=p_send.at[i], recv_sem=p_recv.at[i],
            device_id={"cp": right}, device_id_type=MESH,
        )

    def send_halo(par, hs, t):
        @pl.when(jnp.logical_not(last))
        def _():
            halo_copy(par, hs, t).start()

        if t == 0:

            @pl.when(first)
            def _():
                own_copy(par, hs, 0).start()
                own_copy(par, hs, 1).start()

    barrier = pltpu.get_barrier_semaphore()
    for peer in peers:
        pl.semaphore_signal(barrier, inc=1, device_id={"cp": peer}, device_id_type=MESH)
    x_copies = [pltpu.make_async_copy(x_hbm.at[t], x_in.at[t], x_sem.at[t]) for t in range(N_FR)]
    for t in (1, 0):
        x_copies[t].start()
    for k in (2, 1, 0):
        w_copy(0, k).start()

    part[...] = jnp.zeros_like(part)
    if EXPLICIT:
        for acc in accs:
            pltpu.matmul_pop(acc)
    else:
        accs[0][...] = jnp.zeros_like(accs[0])
    for b in range(2):
        for f in range(4):
            gains[2 * b, f : f + 1, :] = in_scale[b : b + 1, :]
            shifts[2 * b, f : f + 1, :] = in_shift[b : b + 1, :]
        gains[2 * b + 1, 2:4, :] = mid_scale[b]
        shifts[2 * b + 1, 2:4, :] = mid_shift[b]
    for t in (1, 0):
        x_copies[t].wait()
        for p in range(N_ROW):
            val = x_in[t, p].astype(F32)
            for half in range(2):
                add_moments(val[:, half * HALF : (half + 1) * HALF], half)
    finish_moments(0)
    pl.semaphore_wait(barrier, cp_size - 1)
    for d in range(cp_size - 1):
        st_copy(0, d).start()

    for t in (1, 0):
        for p in range(N_ROW):
            val = x_in[t, p].astype(F32)
            for j in range(4):
                tmp[p % 2, j] = val[:, j * 128 : (j + 1) * 128]
            for j in range(4):
                for v in range(N_TILE):
                    raw[0, t, p, v * TILE : (v + 1) * TILE, j * 128 : (j + 1) * 128] = tmp[
                        p % 2, j, pl.ds(v, TILE, stride=N_TILE), :
                    ].astype(BF16)
        if t == 1:

            @pl.when(jnp.logical_not(last))
            def _():
                for i in range(2):
                    param_copy(i).start()

        send_halo(0, 0, t)

    def conv(c, carry):
        par = lax.rem(c, 2)
        nxt = 1 - par

        @pl.when(c < N_CONV - 1)
        def _():
            for k in (2, 1, 0):
                w_copy(c + 1, k).start()

        for d in range(cp_size - 1):
            st_copy(par, d).wait()
        statistics(par)

        def own(t):
            return lambda p, cut: raw[par, t, p, :, cut]

        def received(t):
            return lambda p, cut: halo[par, t, p, :, cut]

        def norms(read, f, halves=(0, 1)):
            return [functools.partial(norm, read, c, f, p, h) for h in halves for p in range(N_ROW)]

        def epilogues(t, rows):
            return [functools.partial(epilogue, c, par, t, p, m) for p in rows for m in range(2)]

        for thunk in norms(own(1), 3, (0,)):
            thunk()
        w_copy(c, 2).wait()
        run(par, steps_of(1, 2, (0,)), norms(own(1), 3, (1,)), 0.9)
        run(par, steps_of(1, 2, (1,)), norms(own(0), 2))
        w_copy(c, 1).wait()

        @pl.when(c == 0)
        def _():
            @pl.when(jnp.logical_not(first))
            def _():
                for i in range(2):
                    param_copy(i).wait_recv()
                for b in range(2):
                    gains[2 * b + 1, 0:2, :] = h_scale[b]
                    shifts[2 * b + 1, 0:2, :] = h_shift[b]

            @pl.when(first)
            def _():
                for b in range(2):
                    for f in range(2):
                        gains[2 * b + 1, f : f + 1, :] = mid_scale[b, 0:1]
                        shifts[2 * b + 1, f : f + 1, :] = mid_shift[b, 0:1]

            @pl.when(jnp.logical_not(last))
            def _():
                for i in range(2):
                    param_copy(i).wait_send()

        own_copy(par, par, 1).wait()
        run(par, steps_of(1, 1), norms(received(1), 1))
        w_copy(c, 0).wait()
        run(par, steps_of(1, 0))
        steps = steps_of(0, 2)
        run(par, steps[:6], epilogues(1, range(N_ROW)))

        @pl.when(jnp.logical_not(last))
        def _():
            halo_copy(par, par, 1).wait_send()
            halo_copy(par, par, 0).wait_send()

        @pl.when(c < N_CONV - 1)
        def _():
            send_halo(nxt, nxt, 1)

        run(par, steps[6:])
        own_copy(par, par, 0).wait()
        run(par, steps_of(0, 1), norms(received(0), 0))
        run(par, steps_of(0, 0, rows=(0, 1)))
        run(par, steps_of(0, 0, rows=(2, 3)), epilogues(0, (0, 1)), 0.8)
        for thunk in epilogues(0, (2, 3)):
            thunk()
        finish_moments(nxt)

        @pl.when(c < N_CONV - 1)
        def _():
            for d in range(cp_size - 1):
                st_copy(nxt, d).start()
            send_halo(nxt, nxt, 0)

        return carry

    lax.fori_loop(0, N_CONV, conv, 0)

    copies = []
    for t in (1, 0):
        for p in range(N_ROW):
            for j in range(4):
                for v in range(N_TILE):
                    tmp[p % 2, j, pl.ds(v, TILE, stride=N_TILE), :] = raw[
                        0, t, p, v * TILE : (v + 1) * TILE, j * 128 : (j + 1) * 128
                    ].astype(F32)
                x_in[t, p, :, j * 128 : (j + 1) * 128] = tmp[p % 2, j].astype(BF16)
            copies.append(pltpu.make_async_copy(x_in.at[t, p], out_hbm.at[t, p], o_sem.at[t, p]))
            copies[-1].start()
    for copy in copies:
        copy.wait()


def solution(mesh):
    cp_size = mesh.shape["cp"]

    def local_decode(latent, conv_w, conv_b, in_scale, in_shift, mid_scale, mid_shift):
        any_spec, vmem = pl.BlockSpec(memory_space=pl.ANY), pl.BlockSpec(memory_space=pltpu.VMEM)
        dma = pltpu.SemaphoreType.DMA
        frame = (N_ROW, N_COL, N_CH)
        extra = [] if EXPLICIT else [pltpu.VMEM((N_FR, N_ROW, 2, N_COL, HALF), F32)]
        return pl.pallas_call(
            functools.partial(kernel, cp_size),
            out_shape=jax.ShapeDtypeStruct(latent.shape, BF16),
            in_specs=[any_spec, any_spec, vmem, vmem, vmem, vmem, vmem],
            out_specs=any_spec,
            scratch_shapes=[
                pltpu.VMEM((N_FR, *frame), BF16),
                pltpu.VMEM((2, N_FR, *frame), BF16),
                pltpu.VMEM((2, N_FR, *frame), BF16),
                pltpu.VMEM((4, N_ROW, PAD_COL, N_CH), BF16),
                pltpu.VMEM((2, 3, 9 * N_CH, N_CH), BF16),
                pltpu.VMEM((2, 8, N_CH), F32),
                pltpu.VMEM((2, 8, 128), F32),
                pltpu.VMEM((2, cp_size - 1, 8, 128), F32),
                pltpu.VMEM((N_CONV, 4, N_CH), F32),
                pltpu.VMEM((N_CONV, 4, N_CH), F32),
                pltpu.VMEM((2, N_FR, N_CH), F32),
                pltpu.VMEM((2, N_FR, N_CH), F32),
                pltpu.VMEM((1, N_CH), F32),
                pltpu.VMEM((1, N_CH), F32),
                pltpu.VMEM((2, 4, N_COL, 128), F32),
                dma((N_FR,)),
                dma((2, 3)),
                dma((2, cp_size - 1)),
                dma((2, cp_size - 1)),
                dma((N_FR,)),
                dma((2, N_FR)),
                dma((2,)),
                dma((2,)),
                dma((N_FR, N_ROW)),
                *extra,
            ],
            compiler_params=pltpu.CompilerParams(
                collective_id=0, has_side_effects=True, vmem_limit_bytes=60 * 1024 * 1024
            ),
        )(latent, conv_w.reshape(N_CONV, 3, 9 * N_CH, N_CH), conv_b, in_scale, in_shift, mid_scale, mid_shift)

    time_spec = P(("dp", "cp"))
    param_spec = P(None, ("dp", "cp"))
    return jax.shard_map(
        local_decode,
        mesh=mesh,
        in_specs=(time_spec, P(), P(), P(), P(), param_spec, param_spec),
        out_specs=time_spec,
        check_vma=False,
    )
```

profile of v0, /device:TPU:0, one launch (start us, length us, event | category | flops | bytes accessed | tf_op | source)
XLA Modules:
  0.0 78.5 jit_solution(8243259798159045425)
XLA Ops:
  0.0 76.3 %shard_map.73 = bf16[2,4,128,512]{3,2,1,0:T(8,128)(2,1)} custom-call(bf16[2,4,128,512]{3,2,1,0:T(8,128)(2,1)} %x_hbm.1, bf16[4,3,4608,512]{3,2,1,0:T(8,128)(2,1)} %bitcast.1, f32[4,512]{1,0:T(4,128)} %bias_ref.1, f32[2,512]{1,0:T(2,128)} %in_scale.1, f32[2,512]{1,0:T(2,128)} %in_shift.1, f32[2,2,512]{2,1,0:T(2,128)} %mid_scale.1, f32[2,2,512]{2,1,0:T(2,128)} %mid_shift.1), custom_call_target="tpu_custom_call" | custom-call | tf_op jit(solution)/shard_map/pallas_call | solution.py:358
  76.3 2.3 %copy.9 = bf16[2,4,128,512]{3,2,1,0:T(8,128)(2,1)} copy(bf16[2,4,128,512]{3,2,1,0:T(8,128)(2,1)} %shard_map.73) | data formatting | bytes 2097152
where the time goes:
time: 78.7 us; the launch traced here: 78.5 us
  Pallas kernels  76.3 us (97%)
  local copies, waits for them, and re-layouts  2.26 us (3%)
    pallas_call x1, Pallas kernels, local_decode(): pl.pallas_call(functools.partial(kernel, cp_size), out_shape=jax.ShapeDty...  76.3 us
    unnamed x1, local copies, waits for them, and re-layouts  2.26 us

commit v1 on v0

--- a/solution.py
+++ b/solution.py
@@ -9,7 +9,6 @@
 
 NUM_GROUPS = 32
 EPSILON = 1e-6
-EXPLICIT = False
 MESH = pl.DeviceIdType.MESH
 F32 = jnp.float32
 BF16 = jnp.bfloat16
@@ -26,35 +25,9 @@
 
 
 def kernel(
-    cp_size,
-    x_hbm, w_hbm, bias_ref, in_scale, in_shift, mid_scale, mid_shift,
-    out_hbm,
-    x_in, raw, halo, act, wts, part, tx, rx, gains, shifts, h_scale, h_shift, mean_ref, rstd_ref, tmp,
+    cp_size, x_hbm, w_hbm, bias_ref, in_scale, in_shift, mid_scale, mid_shift, out_hbm,
+    x_in, raw, halo, act, wts, acc, part, tx, rx, gains, shifts, h_scale, h_shift, coef, tmp,
     x_sem, w_sem, st_send, st_recv, h_send, h_recv, p_send, p_recv, o_sem,
-    *extra,
-):
-    if EXPLICIT:
-        pl.run_scoped(
-            functools.partial(
-                body, cp_size, x_hbm, w_hbm, bias_ref, in_scale, in_shift, mid_scale, mid_shift, out_hbm,
-                x_in, raw, halo, act, wts, part, tx, rx, gains, shifts, h_scale, h_shift, mean_ref, rstd_ref, tmp,
-                x_sem, w_sem, st_send, st_recv, h_send, h_recv, p_send, p_recv, o_sem,
-            ),
-            *[pltpu.ACC(m)((N_COL, HALF), F32) for m in range(2) for _ in range(N_FR * N_ROW)],
-        )
-    else:
-        body(
-            cp_size, x_hbm, w_hbm, bias_ref, in_scale, in_shift, mid_scale, mid_shift, out_hbm,
-            x_in, raw, halo, act, wts, part, tx, rx, gains, shifts, h_scale, h_shift, mean_ref, rstd_ref, tmp,
-            x_sem, w_sem, st_send, st_recv, h_send, h_recv, p_send, p_recv, o_sem, *extra,
-        )
-
-
-def body(
-    cp_size, x_hbm, w_hbm, bias_ref, in_scale, in_shift, mid_scale, mid_shift, out_hbm,
-    x_in, raw, halo, act, wts, part, tx, rx, gains, shifts, h_scale, h_shift, mean_ref, rstd_ref, tmp,
-    x_sem, w_sem, st_send, st_recv, h_send, h_recv, p_send, p_recv, o_sem,
-    *accs,
 ):
     cp = lax.axis_index("cp")
     count = float(N_FR * cp_size * N_ROW * N_COL * (N_CH // NUM_GROUPS))
@@ -62,43 +35,32 @@
     peers = [lax.rem(cp + d, cp_size) for d in range(1, cp_size)]
     right = lax.rem(cp + 1, cp_size)
 
-    def acc_of(m, t, p):
-        return accs[(m * N_FR + t) * N_ROW + p]
-
-    def mm_push(slot, k, dp, dq, kt, m, reg):
+    def mm_step(slot, t, k, p, dp, dq, kt):
+        lhs = act[t + k, p + dp, TILE * (1 + dq) : TILE * (1 + dq) + N_COL, kt * HALF : (kt + 1) * HALF]
         off = ((dp + 1) * 3 + dq + 1) * N_CH + kt * HALF
-        w = wts[slot, k, off : off + HALF, m * HALF : (m + 1) * HALF]
-        pltpu.matmul_push_rhs(w, staging_register=reg, mxu_index=m)
-
-    def mm_step(slot, t, k, dp, dq, kt, rows, reg):
-        rows = [p for p in rows if 0 <= p + dp < N_ROW]
-        if EXPLICIT:
-            for m in range(2):
-                mm_push(slot, k, dp, dq, kt, m, reg)
-        for i, p in enumerate(rows):
-            lhs = act[t + k, p + dp, TILE * (1 + dq) : TILE * (1 + dq) + N_COL, kt * HALF : (kt + 1) * HALF]
-            for m in range(2):
-                if EXPLICIT:
-                    pltpu.matmul_acc_lhs(acc_of(m, t, p), lhs, load_staged_rhs=reg if i == 0 else None)
-                else:
-                    off = ((dp + 1) * 3 + dq + 1) * N_CH + kt * HALF
-                    w = wts[slot, k, off : off + HALF, m * HALF : (m + 1) * HALF]
-                    accs[0][t, p, m] += jnp.dot(lhs, w, preferred_element_type=F32)
+        for m in range(2):
+            w = wts[slot, k, off : off + HALF, m * HALF : (m + 1) * HALF]
+            acc[t, p, m] += jnp.dot(lhs, w, preferred_element_type=F32)
 
     def pop(m, t, p):
-        if EXPLICIT:
-            return pltpu.matmul_pop(acc_of(m, t, p))
-        val = accs[0][t, p, m]
-        accs[0][t, p, m] = jnp.zeros((N_COL, HALF), F32)
+        val = acc[t, p, m]
+        acc[t, p, m] = jnp.zeros((N_COL, HALF), F32)
         return val
 
     def steps_of(t, k, kts=(0, 1), rows=range(N_ROW)):
-        return [(t, k, dp, dq, kt, tuple(rows)) for kt in kts for dp in (0, -1, 1) for dq in (0, -1, 1)]
+        return [
+            (t, k, p, dp, dq, kt)
+            for kt in kts
+            for p in rows
+            for dp in (0, 1, -1)
+            if 0 <= p + dp < N_ROW
+            for dq in (0, -1, 1)
+        ]
 
     def run(slot, steps, thunks=(), upto=1.0):
         done, span = 0, max(1, int(len(steps) * upto))
-        for i, (t, k, dp, dq, kt, rows) in enumerate(steps):
-            mm_step(slot, t, k, dp, dq, kt, rows, i % 2)
+        for i, step in enumerate(steps):
+            mm_step(slot, *step)
             want = min(len(thunks), -(-len(thunks) * (i + 1) // span))
             for thunk in thunks[done:want]:
                 thunk()
@@ -110,11 +72,10 @@
         part[0, :, cut] += jnp.sum(rows, axis=0)
         part[1, :, cut] += jnp.sum(rows * rows, axis=0)
 
-    def norm(read, c, f, p, half):
+    def norm(read, f, p, half):
         cut = slice(half * HALF, (half + 1) * HALF)
-        gain = rstd_ref[0:1, cut] * gains[c, f : f + 1, cut]
-        val = (read(p, cut).astype(F32) - mean_ref[0:1, cut]) * gain + shifts[c, f : f + 1, cut]
-        val = 0.5 * val.astype(BF16).astype(F32)
+        val = read(p, cut).astype(F32) * coef[0, f : f + 1, cut] + coef[1, f : f + 1, cut]
+        val = val.astype(BF16).astype(F32)
         val = val + val * jnp.tanh(val)
         act[f, p, TILE : TILE + N_COL, cut] = val.astype(BF16)
         row = lax.broadcasted_iota(jnp.int32, (TILE, HALF), 0)
@@ -125,9 +86,8 @@
 
     def epilogue(c, par, t, p, m):
         cut = slice(m * HALF, (m + 1) * HALF)
-        flag = par.astype(F32)
         conv = (pop(m, t, p) + bias_ref[pl.ds(c, 1), cut]).astype(BF16).astype(F32)
-        val = (raw[0, t, p, :, cut].astype(F32) * flag + conv).astype(BF16)
+        val = (raw[2 - 2 * par, t, p, :, cut].astype(F32) + conv).astype(BF16)
         raw[1 - par, t, p, :, cut] = val
         add_moments(val.astype(F32), m)
 
@@ -143,16 +103,27 @@
         for d in range(cp_size - 1):
             total = total + rx[slot, d]
         lane = lax.broadcasted_iota(jnp.int32, total.shape, 1)
-        for shift in (1, 2, 4, 8):
-            total = total + jnp.where(
-                (lane & shift) == 0, pltpu.roll(total, 128 - shift, 1), pltpu.roll(total, shift, 1)
-            )
-        mean = total[0:4] / count
-        var = total[4:8] / count - mean * mean
-        rstd = lax.rsqrt(var + EPSILON)
+        for unit in (1, 4):
+            spot = (lane // unit) % 4
+            terms = [total]
+            for d in range(1, 4):
+                up, down = pltpu.roll(total, 128 - d * unit, 1), pltpu.roll(total, d * unit, 1)
+                terms.append(jnp.where(spot < 4 - d, up, 0.0))
+                terms.append(jnp.where(spot >= d, down, 0.0))
+            while len(terms) > 1:
+                terms = [terms[i] + terms[i + 1] for i in range(0, len(terms) - 1, 2)] + terms[len(terms) & ~1 :]
+            total = terms[0]
+        mean = total[0:4] * (1.0 / count)
+        var = total[4:8] * (1.0 / count) - mean * mean
+        return mean, lax.rsqrt(var + EPSILON)
+
+    def coefficients(c, mean, rstd, frames):
         for j in range(4):
-            mean_ref[0:1, j * 128 : (j + 1) * 128] = mean[j : j + 1]
-            rstd_ref[0:1, j * 128 : (j + 1) * 128] = rstd[j : j + 1]
+            cut = slice(j * 128, (j + 1) * 128)
+            for f in frames:
+                gain = 0.5 * (rstd[j : j + 1] * gains[c, f : f + 1, cut])
+                coef[0, f : f + 1, cut] = gain
+                coef[1, f : f + 1, cut] = 0.5 * shifts[c, f : f + 1, cut] - mean[j : j + 1] * gain
 
     def w_copy(c, k):
         slot = lax.rem(c, 2)
@@ -202,11 +173,8 @@
         w_copy(0, k).start()
 
     part[...] = jnp.zeros_like(part)
-    if EXPLICIT:
-        for acc in accs:
-            pltpu.matmul_pop(acc)
-    else:
-        accs[0][...] = jnp.zeros_like(accs[0])
+    acc[...] = jnp.zeros_like(acc)
+    raw[2] = jnp.zeros((N_FR, N_ROW, N_COL, N_CH), BF16)
     for b in range(2):
         for f in range(4):
             gains[2 * b, f : f + 1, :] = in_scale[b : b + 1, :]
@@ -254,7 +222,8 @@
 
         for d in range(cp_size - 1):
             st_copy(par, d).wait()
-        statistics(par)
+        mean, rstd = statistics(par)
+        coefficients(c, mean, rstd, (3, 2))
 
         def own(t):
             return lambda p, cut: raw[par, t, p, :, cut]
@@ -263,17 +232,13 @@
             return lambda p, cut: halo[par, t, p, :, cut]
 
         def norms(read, f, halves=(0, 1)):
-            return [functools.partial(norm, read, c, f, p, h) for h in halves for p in range(N_ROW)]
+            return [functools.partial(norm, read, f, p, h) for h in halves for p in range(N_ROW)]
 
         def epilogues(t, rows):
             return [functools.partial(epilogue, c, par, t, p, m) for p in rows for m in range(2)]
 
         for thunk in norms(own(1), 3, (0,)):
             thunk()
-        w_copy(c, 2).wait()
-        run(par, steps_of(1, 2, (0,)), norms(own(1), 3, (1,)), 0.9)
-        run(par, steps_of(1, 2, (1,)), norms(own(0), 2))
-        w_copy(c, 1).wait()
 
         @pl.when(c == 0)
         def _():
@@ -297,12 +262,20 @@
                 for i in range(2):
                     param_copy(i).wait_send()
 
+        coefficients(c, mean, rstd, (1, 0))
+        w_copy(c, 2).wait()
+        run(par, steps_of(1, 2, (0,)), norms(own(1), 3, (1,)), 0.9)
+        run(par, steps_of(1, 2, (1,)), norms(own(0), 2))
+        w_copy(c, 1).wait()
+        steps = steps_of(1, 1)
+        run(par, steps[:44])
         own_copy(par, par, 1).wait()
-        run(par, steps_of(1, 1), norms(received(1), 1))
+        run(par, steps[44:], norms(received(1), 1))
         w_copy(c, 0).wait()
-        run(par, steps_of(1, 0))
+        for p in range(N_ROW):
+            run(par, steps_of(1, 0, rows=(p,)), epilogues(1, (p - 1,)) if p else ())
         steps = steps_of(0, 2)
-        run(par, steps[:6], epilogues(1, range(N_ROW)))
+        run(par, steps[:10], epilogues(1, (N_ROW - 1,)))
 
         @pl.when(jnp.logical_not(last))
         def _():
@@ -313,12 +286,14 @@
         def _():
             send_halo(nxt, nxt, 1)
 
-        run(par, steps[6:])
+        run(par, steps[10:])
+        steps = steps_of(0, 1)
+        run(par, steps[:40])
         own_copy(par, par, 0).wait()
-        run(par, steps_of(0, 1), norms(received(0), 0))
-        run(par, steps_of(0, 0, rows=(0, 1)))
-        run(par, steps_of(0, 0, rows=(2, 3)), epilogues(0, (0, 1)), 0.8)
-        for thunk in epilogues(0, (2, 3)):
+        run(par, steps[40:], norms(received(0), 0))
+        for p in range(N_ROW):
+            run(par, steps_of(0, 0, rows=(p,)), epilogues(0, (p - 1,)) if p else ())
+        for thunk in epilogues(0, (N_ROW - 1,)):
             thunk()
         finish_moments(nxt)
 
@@ -354,7 +329,6 @@
         any_spec, vmem = pl.BlockSpec(memory_space=pl.ANY), pl.BlockSpec(memory_space=pltpu.VMEM)
         dma = pltpu.SemaphoreType.DMA
         frame = (N_ROW, N_COL, N_CH)
-        extra = [] if EXPLICIT else [pltpu.VMEM((N_FR, N_ROW, 2, N_COL, HALF), F32)]
         return pl.pallas_call(
             functools.partial(kernel, cp_size),
             out_shape=jax.ShapeDtypeStruct(latent.shape, BF16),
@@ -362,10 +336,11 @@
             out_specs=any_spec,
             scratch_shapes=[
                 pltpu.VMEM((N_FR, *frame), BF16),
-                pltpu.VMEM((2, N_FR, *frame), BF16),
+                pltpu.VMEM((3, N_FR, *frame), BF16),
                 pltpu.VMEM((2, N_FR, *frame), BF16),
                 pltpu.VMEM((4, N_ROW, PAD_COL, N_CH), BF16),
                 pltpu.VMEM((2, 3, 9 * N_CH, N_CH), BF16),
+                pltpu.VMEM((N_FR, N_ROW, 2, N_COL, HALF), F32),
                 pltpu.VMEM((2, 8, N_CH), F32),
                 pltpu.VMEM((2, 8, 128), F32),
                 pltpu.VMEM((2, cp_size - 1, 8, 128), F32),
@@ -373,8 +348,7 @@
                 pltpu.VMEM((N_CONV, 4, N_CH), F32),
                 pltpu.VMEM((2, N_FR, N_CH), F32),
                 pltpu.VMEM((2, N_FR, N_CH), F32),
-                pltpu.VMEM((1, N_CH), F32),
-                pltpu.VMEM((1, N_CH), F32),
+                pltpu.VMEM((2, 4, N_CH), F32),
                 pltpu.VMEM((2, 4, N_COL, 128), F32),
                 dma((N_FR,)),
                 dma((2, 3)),
@@ -385,7 +359,6 @@
                 dma((2,)),
                 dma((2,)),
                 dma((N_FR, N_ROW)),
-                *extra,
             ],
             compiler_params=pltpu.CompilerParams(
                 collective_id=0, has_side_effects=True, vmem_limit_bytes=60 * 1024 * 1024

time: 78.7 us -> 74.6 us (0.948)
  Pallas kernels: 76.3 us -> 72.2 us
    pallas_call x1, Pallas kernels: 76.3 us -> 72.2 us  [local_decode(): pl.pallas_call(functools.partial(kernel, cp_size), out_shape=jax.ShapeDty...]
where the time goes in v1:
time: 74.6 us; the launch traced here: 74.5 us
  Pallas kernels  72.2 us (97%)
  local copies, waits for them, and re-layouts  2.26 us (3%)
    pallas_call x1, Pallas kernels, local_decode(): pl.pallas_call(functools.partial(kernel, cp_size), out_shape=jax.ShapeDty...  72.2 us
    unnamed x1, local copies, waits for them, and re-layouts  2.26 us

profile of v1, /device:TPU:0, one launch (start us, length us, event | category | flops | bytes accessed | tf_op | source)
XLA Modules:
  0.0 74.5 jit_solution(5336914236471741821)
XLA Ops:
  0.0 72.2 %shard_map.73 = bf16[2,4,128,512]{3,2,1,0:T(8,128)(2,1)} custom-call(bf16[2,4,128,512]{3,2,1,0:T(8,128)(2,1)} %x_hbm.1, bf16[4,3,4608,512]{3,2,1,0:T(8,128)(2,1)} %bitcast.1, f32[4,512]{1,0:T(4,128)} %bias_ref.1, f32[2,512]{1,0:T(2,128)} %in_scale.1, f32[2,512]{1,0:T(2,128)} %in_shift.1, f32[2,2,512]{2,1,0:T(2,128)} %mid_scale.1, f32[2,2,512]{2,1,0:T(2,128)} %mid_shift.1), custom_call_target="tpu_custom_call" | custom-call | tf_op jit(solution)/shard_map/pallas_call | solution.py:332
  72.2 2.3 %copy.9 = bf16[2,4,128,512]{3,2,1,0:T(8,128)(2,1)} copy(bf16[2,4,128,512]{3,2,1,0:T(8,128)(2,1)} %shard_map.73) | data formatting | bytes 2097152

commit v2 on v1

--- a/solution.py
+++ b/solution.py
@@ -19,15 +19,17 @@
 N_COL = 128
 N_CH = 512
 TILE = 16
+PIECES = ((1, slice(0, 2)), (1, slice(2, 4)), (0, slice(0, 4)))
 N_TILE = N_COL // TILE
 PAD_COL = N_COL + 2 * TILE
 HALF = 256
 
 
 def kernel(
-    cp_size, x_hbm, w_hbm, bias_ref, in_scale, in_shift, mid_scale, mid_shift, out_hbm,
+    cp_size, x_hbm, w_hbm, bias_hbm, in_scale_hbm, in_shift_hbm, mid_scale_hbm, mid_shift_hbm, out_ref,
+    bias_ref, in_scale, in_shift, mid_scale, mid_shift,
     x_in, raw, halo, act, wts, acc, part, tx, rx, gains, shifts, h_scale, h_shift, coef, tmp,
-    x_sem, w_sem, st_send, st_recv, h_send, h_recv, p_send, p_recv, o_sem,
+    x_sem, s_sem, w_sem, st_send, st_recv, h_send, h_recv, p_send, p_recv,
 ):
     cp = lax.axis_index("cp")
     count = float(N_FR * cp_size * N_ROW * N_COL * (N_CH // NUM_GROUPS))
@@ -135,14 +137,17 @@
             device_id={"cp": peers[d]}, device_id_type=MESH,
         )
 
-    def halo_copy(par, hs, t):
+    def halo_copy(par, hs, i):
+        t, rows = PIECES[i]
         return pltpu.make_async_remote_copy(
-            src_ref=raw.at[par, t], dst_ref=halo.at[hs, t], send_sem=h_send.at[t], recv_sem=h_recv.at[hs, t],
+            src_ref=raw.at[par, t, rows], dst_ref=halo.at[hs, t, rows],
+            send_sem=h_send.at[hs, i], recv_sem=h_recv.at[hs, i],
             device_id={"cp": right}, device_id_type=MESH,
         )
 
-    def own_copy(par, hs, t):
-        return pltpu.make_async_copy(raw.at[par, 0], halo.at[hs, t], h_recv.at[hs, t])
+    def own_copy(par, hs, i):
+        t, rows = PIECES[i]
+        return pltpu.make_async_copy(raw.at[par, 0, rows], halo.at[hs, t, rows], h_recv.at[hs, i])
 
     def param_copy(i):
         src, dst = ((mid_scale, h_scale), (mid_shift, h_shift))[i]
@@ -151,36 +156,23 @@
             device_id={"cp": right}, device_id_type=MESH,
         )
 
-    def send_halo(par, hs, t):
-        @pl.when(jnp.logical_not(last))
-        def _():
-            halo_copy(par, hs, t).start()
-
-        if t == 0:
-
-            @pl.when(first)
-            def _():
-                own_copy(par, hs, 0).start()
-                own_copy(par, hs, 1).start()
-
     barrier = pltpu.get_barrier_semaphore()
     for peer in peers:
         pl.semaphore_signal(barrier, inc=1, device_id={"cp": peer}, device_id_type=MESH)
     x_copies = [pltpu.make_async_copy(x_hbm.at[t], x_in.at[t], x_sem.at[t]) for t in range(N_FR)]
     for t in (1, 0):
         x_copies[t].start()
+    small = ((bias_hbm, bias_ref), (in_scale_hbm, in_scale), (in_shift_hbm, in_shift),
+             (mid_scale_hbm, mid_scale), (mid_shift_hbm, mid_shift))
+    small_copies = [pltpu.make_async_copy(src, dst, s_sem.at[i]) for i, (src, dst) in enumerate(small)]
+    for copy in small_copies:
+        copy.start()
     for k in (2, 1, 0):
         w_copy(0, k).start()
 
     part[...] = jnp.zeros_like(part)
     acc[...] = jnp.zeros_like(acc)
     raw[2] = jnp.zeros((N_FR, N_ROW, N_COL, N_CH), BF16)
-    for b in range(2):
-        for f in range(4):
-            gains[2 * b, f : f + 1, :] = in_scale[b : b + 1, :]
-            shifts[2 * b, f : f + 1, :] = in_shift[b : b + 1, :]
-        gains[2 * b + 1, 2:4, :] = mid_scale[b]
-        shifts[2 * b + 1, 2:4, :] = mid_shift[b]
     for t in (1, 0):
         x_copies[t].wait()
         for p in range(N_ROW):
@@ -192,6 +184,14 @@
     for d in range(cp_size - 1):
         st_copy(0, d).start()
 
+    for copy in small_copies:
+        copy.wait()
+    for b in range(2):
+        for f in range(4):
+            gains[2 * b, f : f + 1, :] = in_scale[b : b + 1, :]
+            shifts[2 * b, f : f + 1, :] = in_shift[b : b + 1, :]
+        gains[2 * b + 1, 2:4, :] = mid_scale[b]
+        shifts[2 * b + 1, 2:4, :] = mid_shift[b]
     for t in (1, 0):
         for p in range(N_ROW):
             val = x_in[t, p].astype(F32)
@@ -202,14 +202,20 @@
                     raw[0, t, p, v * TILE : (v + 1) * TILE, j * 128 : (j + 1) * 128] = tmp[
                         p % 2, j, pl.ds(v, TILE, stride=N_TILE), :
                     ].astype(BF16)
-        if t == 1:
-
-            @pl.when(jnp.logical_not(last))
-            def _():
-                for i in range(2):
-                    param_copy(i).start()
-
-        send_halo(0, 0, t)
+            if (t, p) in ((1, 1), (1, 3), (0, 3)):
+                piece = {(1, 1): 0, (1, 3): 1, (0, 3): 2}[t, p]
+
+                @pl.when(jnp.logical_not(last))
+                def _():
+                    if piece == 0:
+                        for i in range(2):
+                            param_copy(i).start()
+                    halo_copy(0, 0, piece).start()
+
+    @pl.when(first)
+    def _():
+        for i in range(3):
+            own_copy(0, 0, i).start()
 
     def conv(c, carry):
         par = lax.rem(c, 2)
@@ -231,8 +237,8 @@
         def received(t):
             return lambda p, cut: halo[par, t, p, :, cut]
 
-        def norms(read, f, halves=(0, 1)):
-            return [functools.partial(norm, read, f, p, h) for h in halves for p in range(N_ROW)]
+        def norms(read, f, halves=(0, 1), rows=range(N_ROW)):
+            return [functools.partial(norm, read, f, p, h) for h in halves for p in rows]
 
         def epilogues(t, rows):
             return [functools.partial(epilogue, c, par, t, p, m) for p in rows for m in range(2)]
@@ -264,32 +270,27 @@
 
         coefficients(c, mean, rstd, (1, 0))
         w_copy(c, 2).wait()
+        w_copy(c, 1).wait()
         run(par, steps_of(1, 2, (0,)), norms(own(1), 3, (1,)), 0.9)
         run(par, steps_of(1, 2, (1,)), norms(own(0), 2))
-        w_copy(c, 1).wait()
-        steps = steps_of(1, 1)
-        run(par, steps[:44])
+        run(par, steps_of(1, 1))
+        w_copy(c, 0).wait()
+        own_copy(par, par, 0).wait()
+        run(par, steps_of(0, 2, (0,)), norms(received(1), 1, rows=(0, 1)))
         own_copy(par, par, 1).wait()
-        run(par, steps[44:], norms(received(1), 1))
-        w_copy(c, 0).wait()
-        for p in range(N_ROW):
-            run(par, steps_of(1, 0, rows=(p,)), epilogues(1, (p - 1,)) if p else ())
-        steps = steps_of(0, 2)
-        run(par, steps[:10], epilogues(1, (N_ROW - 1,)))
-
-        @pl.when(jnp.logical_not(last))
+        run(par, steps_of(1, 0, rows=(0,)), norms(received(1), 1, rows=(2, 3)), 0.7)
+        for p in (1, 2):
+            run(par, steps_of(1, 0, rows=(p,)), epilogues(1, (p - 1,)), 0.6)
+
+        @pl.when(jnp.logical_and(c < N_CONV - 1, jnp.logical_not(last)))
         def _():
-            halo_copy(par, par, 1).wait_send()
-            halo_copy(par, par, 0).wait_send()
-
-        @pl.when(c < N_CONV - 1)
-        def _():
-            send_halo(nxt, nxt, 1)
-
-        run(par, steps[10:])
+            halo_copy(nxt, nxt, 0).start()
+
+        run(par, steps_of(1, 0, rows=(3,)), epilogues(1, (2,)))
+        run(par, steps_of(0, 2, (1,)), epilogues(1, (3,)))
         steps = steps_of(0, 1)
         run(par, steps[:40])
-        own_copy(par, par, 0).wait()
+        own_copy(par, par, 2).wait()
         run(par, steps[40:], norms(received(0), 0))
         for p in range(N_ROW):
             run(par, steps_of(0, 0, rows=(p,)), epilogues(0, (p - 1,)) if p else ())
@@ -301,22 +302,41 @@
         def _():
             for d in range(cp_size - 1):
                 st_copy(nxt, d).start()
-            send_halo(nxt, nxt, 0)
+
+            @pl.when(jnp.logical_not(last))
+            def _():
+                for i in (1, 2):
+                    halo_copy(nxt, nxt, i).start()
+
+            @pl.when(first)
+            def _():
+                for i in range(3):
+                    own_copy(nxt, nxt, i).start()
+
+        @pl.when(jnp.logical_not(last))
+        def _():
+            for i in range(3):
+                halo_copy(par, par, i).wait_send()
 
         return carry
 
     lax.fori_loop(0, N_CONV, conv, 0)
 
+    out_ref[...] = raw[0]
+
+
+def reorder(val_ref, out_hbm, tmp, buf, sem):
     copies = []
-    for t in (1, 0):
+    for t in range(N_FR):
         for p in range(N_ROW):
             for j in range(4):
+                cut = slice(j * 128, (j + 1) * 128)
                 for v in range(N_TILE):
-                    tmp[p % 2, j, pl.ds(v, TILE, stride=N_TILE), :] = raw[
-                        0, t, p, v * TILE : (v + 1) * TILE, j * 128 : (j + 1) * 128
+                    tmp[p % 2, j, pl.ds(v, TILE, stride=N_TILE), :] = val_ref[
+                        t, p, v * TILE : (v + 1) * TILE, cut
                     ].astype(F32)
-                x_in[t, p, :, j * 128 : (j + 1) * 128] = tmp[p % 2, j].astype(BF16)
-            copies.append(pltpu.make_async_copy(x_in.at[t, p], out_hbm.at[t, p], o_sem.at[t, p]))
+                buf[t, p, :, cut] = tmp[p % 2, j].astype(BF16)
+            copies.append(pltpu.make_async_copy(buf.at[t, p], out_hbm.at[t, p], sem.at[t, p]))
             copies[-1].start()
     for copy in copies:
         copy.wait()
@@ -329,12 +349,17 @@
         any_spec, vmem = pl.BlockSpec(memory_space=pl.ANY), pl.BlockSpec(memory_space=pltpu.VMEM)
         dma = pltpu.SemaphoreType.DMA
         frame = (N_ROW, N_COL, N_CH)
-        return pl.pallas_call(
+        blocks = pl.pallas_call(
             functools.partial(kernel, cp_size),
             out_shape=jax.ShapeDtypeStruct(latent.shape, BF16),
-            in_specs=[any_spec, any_spec, vmem, vmem, vmem, vmem, vmem],
-            out_specs=any_spec,
+            in_specs=[any_spec] * 7,
+            out_specs=vmem,
             scratch_shapes=[
+                pltpu.VMEM((N_CONV, N_CH), F32),
+                pltpu.VMEM((2, N_CH), F32),
+                pltpu.VMEM((2, N_CH), F32),
+                pltpu.VMEM((2, N_FR, N_CH), F32),
+                pltpu.VMEM((2, N_FR, N_CH), F32),
                 pltpu.VMEM((N_FR, *frame), BF16),
                 pltpu.VMEM((3, N_FR, *frame), BF16),
                 pltpu.VMEM((2, N_FR, *frame), BF16),
@@ -351,19 +376,36 @@
                 pltpu.VMEM((2, 4, N_CH), F32),
                 pltpu.VMEM((2, 4, N_COL, 128), F32),
                 dma((N_FR,)),
+                dma((5,)),
                 dma((2, 3)),
                 dma((2, cp_size - 1)),
                 dma((2, cp_size - 1)),
-                dma((N_FR,)),
-                dma((2, N_FR)),
+                dma((2, 3)),
+                dma((2, 3)),
                 dma((2,)),
                 dma((2,)),
+            ],
+            compiler_params=pltpu.CompilerParams(
+                collective_id=0, has_side_effects=True, vmem_limit_bytes=46 * 1024 * 1024
+            ),
+        )(*[
+            pltpu.with_memory_space_constraint(arg, pltpu.HBM)
+            for arg in (
+                latent, conv_w.reshape(N_CONV, 3, 9 * N_CH, N_CH), conv_b, in_scale, in_shift, mid_scale, mid_shift
+            )
+        ])
+        return pl.pallas_call(
+            reorder,
+            out_shape=jax.ShapeDtypeStruct(latent.shape, BF16),
+            in_specs=[vmem],
+            out_specs=any_spec,
+            scratch_shapes=[
+                pltpu.VMEM((2, 4, N_COL, 128), F32),
+                pltpu.VMEM((N_FR, *frame), BF16),
                 dma((N_FR, N_ROW)),
             ],
-            compiler_params=pltpu.CompilerParams(
-                collective_id=0, has_side_effects=True, vmem_limit_bytes=60 * 1024 * 1024
-            ),
-        )(latent, conv_w.reshape(N_CONV, 3, 9 * N_CH, N_CH), conv_b, in_scale, in_shift, mid_scale, mid_shift)
+            compiler_params=pltpu.CompilerParams(vmem_limit_bytes=6 * 1024 * 1024),
+        )(blocks)
 
     time_spec = P(("dp", "cp"))
     param_spec = P(None, ("dp", "cp"))

time: 74.6 us -> 71.8 us (0.962)
  local copies, waits for them, and re-layouts: 2.26 us -> 0 us
    unnamed x1 -> x0, local copies, waits for them, and re-layouts: 2.26 us -> none
    pallas_call x1, Pallas kernels: 72.2 us -> 70.5 us  [local_decode(): pl.pallas_call(functools.partial(kernel, cp_size), out_shape=jax.ShapeDty...]
    pallas_call x0 -> x1, Pallas kernels: none -> 1.2 us  [local_decode(): pl.pallas_call(reorder, out_shape=jax.ShapeDtypeStruct(latent.shape, BF16...]
where the time goes in v2:
time: 71.8 us; the launch traced here: 71.7 us
  Pallas kernels  71.7 us (100%)
    pallas_call x1, Pallas kernels, local_decode(): pl.pallas_call(functools.partial(kernel, cp_size), out_shape=jax.ShapeDty...  70.5 us

profile of v2, /device:TPU:0, one launch (start us, length us, event | category | flops | bytes accessed | tf_op | source)
XLA Modules:
  0.0 71.7 jit_solution(15126194245372550248)
XLA Ops:
  0.0 70.5 %shard_map.73.val_ref = bf16[2,4,128,512]{3,2,1,0:T(8,128)(2,1)S(1)} custom-call(bf16[2,4,128,512]{3,2,1,0:T(8,128)(2,1)} %x_hbm.1, bf16[4,3,4608,512]{3,2,1,0:T(8,128)(2,1)} %bitcast.1, f32[4,512]{1,0:T(4,128)} %bias_hbm.1, f32[2,512]{1,0:T(2,128)} %in_scale_hbm.1, f32[2,512]{1,0:T(2,128)} %in_shift_hbm.1, f32[2,2,512]{2,1,0:T(2,128)} %mid_scale_hbm.1, ...), custom_call_target="tpu_custom_call" | custom-call | tf_op jit(solution)/shard_map/pallas_call | solution.py:352
  70.5 1.2 %shard_map.74 = bf16[2,4,128,512]{3,2,1,0:T(8,128)(2,1)} custom-call(bf16[2,4,128,512]{3,2,1,0:T(8,128)(2,1)S(1)} %shard_map.73.val_ref), custom_call_target="tpu_custom_call" | custom-call | tf_op jit(solution)/shard_map/pallas_call | solution.py:397

commit v3 on v2

--- a/solution.py
+++ b/solution.py
@@ -19,7 +19,7 @@
 N_COL = 128
 N_CH = 512
 TILE = 16
-PIECES = ((1, slice(0, 2)), (1, slice(2, 4)), (0, slice(0, 4)))
+PIECES = ((1, slice(0, 2)), (1, slice(2, 4)), (0, slice(0, 2)), (0, slice(2, 4)))
 N_TILE = N_COL // TILE
 PAD_COL = N_COL + 2 * TILE
 HALF = 256
@@ -49,12 +49,12 @@
         acc[t, p, m] = jnp.zeros((N_COL, HALF), F32)
         return val
 
-    def steps_of(t, k, kts=(0, 1), rows=range(N_ROW)):
+    def steps_of(t, k, kts=(0, 1), rows=range(N_ROW), dps=(0, 1, -1)):
         return [
             (t, k, p, dp, dq, kt)
             for kt in kts
             for p in rows
-            for dp in (0, 1, -1)
+            for dp in dps
             if 0 <= p + dp < N_ROW
             for dq in (0, -1, 1)
         ]
@@ -202,8 +202,8 @@
                     raw[0, t, p, v * TILE : (v + 1) * TILE, j * 128 : (j + 1) * 128] = tmp[
                         p % 2, j, pl.ds(v, TILE, stride=N_TILE), :
                     ].astype(BF16)
-            if (t, p) in ((1, 1), (1, 3), (0, 3)):
-                piece = {(1, 1): 0, (1, 3): 1, (0, 3): 2}[t, p]
+            if p % 2:
+                piece = 2 * (1 - t) + p // 2
 
                 @pl.when(jnp.logical_not(last))
                 def _():
@@ -214,7 +214,7 @@
 
     @pl.when(first)
     def _():
-        for i in range(3):
+        for i in range(len(PIECES)):
             own_copy(0, 0, i).start()
 
     def conv(c, carry):
@@ -243,7 +243,7 @@
         def epilogues(t, rows):
             return [functools.partial(epilogue, c, par, t, p, m) for p in rows for m in range(2)]
 
-        for thunk in norms(own(1), 3, (0,)):
+        for thunk in norms(own(1), 3, (0,), (0, 1)):
             thunk()
 
         @pl.when(c == 0)
@@ -271,29 +271,32 @@
         coefficients(c, mean, rstd, (1, 0))
         w_copy(c, 2).wait()
         w_copy(c, 1).wait()
-        run(par, steps_of(1, 2, (0,)), norms(own(1), 3, (1,)), 0.9)
+        run(par, steps_of(1, 2, (0,)), norms(own(1), 3, (0,), (2, 3)) + norms(own(1), 3, (1,)), 0.9)
         run(par, steps_of(1, 2, (1,)), norms(own(0), 2))
         run(par, steps_of(1, 1))
         w_copy(c, 0).wait()
         own_copy(par, par, 0).wait()
-        run(par, steps_of(0, 2, (0,)), norms(received(1), 1, rows=(0, 1)))
+        steps = steps_of(0, 2)
+        run(par, steps[:40], norms(received(1), 1, rows=(0, 1)), 0.9)
         own_copy(par, par, 1).wait()
-        run(par, steps_of(1, 0, rows=(0,)), norms(received(1), 1, rows=(2, 3)), 0.7)
-        for p in (1, 2):
-            run(par, steps_of(1, 0, rows=(p,)), epilogues(1, (p - 1,)), 0.6)
+        run(par, steps[40:], norms(received(1), 1, rows=(2, 3)), 0.9)
+        run(par, steps_of(1, 0, dps=(1, -1)))
+        for p in range(N_ROW):
+            run(par, steps_of(1, 0, rows=(p,), dps=(0,)), epilogues(1, (p - 1,)) if p else ())
+        steps = steps_of(0, 1)
+        run(par, steps[:8], epilogues(1, (3,)))
 
         @pl.when(jnp.logical_and(c < N_CONV - 1, jnp.logical_not(last)))
         def _():
             halo_copy(nxt, nxt, 0).start()
 
-        run(par, steps_of(1, 0, rows=(3,)), epilogues(1, (2,)))
-        run(par, steps_of(0, 2, (1,)), epilogues(1, (3,)))
-        steps = steps_of(0, 1)
-        run(par, steps[:40])
         own_copy(par, par, 2).wait()
-        run(par, steps[40:], norms(received(0), 0))
+        run(par, steps[8:52], norms(received(0), 0, rows=(0, 1)), 0.9)
+        own_copy(par, par, 3).wait()
+        run(par, steps[52:], norms(received(0), 0, rows=(2, 3)), 0.9)
+        run(par, steps_of(0, 0, dps=(1, -1)))
         for p in range(N_ROW):
-            run(par, steps_of(0, 0, rows=(p,)), epilogues(0, (p - 1,)) if p else ())
+            run(par, steps_of(0, 0, rows=(p,), dps=(0,)), epilogues(0, (p - 1,)) if p else ())
         for thunk in epilogues(0, (N_ROW - 1,)):
             thunk()
         finish_moments(nxt)
@@ -305,17 +308,17 @@
 
             @pl.when(jnp.logical_not(last))
             def _():
-                for i in (1, 2):
+                for i in range(1, len(PIECES)):
                     halo_copy(nxt, nxt, i).start()
 
             @pl.when(first)
             def _():
-                for i in range(3):
+                for i in range(len(PIECES)):
                     own_copy(nxt, nxt, i).start()
 
         @pl.when(jnp.logical_not(last))
         def _():
-            for i in range(3):
+            for i in range(len(PIECES)):
                 halo_copy(par, par, i).wait_send()
 
         return carry
@@ -380,8 +383,8 @@
                 dma((2, 3)),
                 dma((2, cp_size - 1)),
                 dma((2, cp_size - 1)),
-                dma((2, 3)),
-                dma((2, 3)),
+                dma((2, len(PIECES))),
+                dma((2, len(PIECES))),
                 dma((2,)),
                 dma((2,)),
             ],

time: 71.8 us -> 69.6 us (0.969)
  Pallas kernels: 71.7 us -> 69.5 us
    pallas_call x1, Pallas kernels: 70.5 us -> 68.3 us  [local_decode(): pl.pallas_call(functools.partial(kernel, cp_size), out_shape=jax.ShapeDty...]
where the time goes in v3:
time: 69.6 us; the launch traced here: 69.5 us
  Pallas kernels  69.5 us (100%)
    pallas_call x1, Pallas kernels, local_decode(): pl.pallas_call(functools.partial(kernel, cp_size), out_shape=jax.ShapeDty...  68.3 us

profile of v3, /device:TPU:0, one launch (start us, length us, event | category | flops | bytes accessed | tf_op | source)
XLA Modules:
  0.0 69.5 jit_solution(9590629496484813787)
XLA Ops:
  0.0 68.3 %shard_map.73.val_ref = bf16[2,4,128,512]{3,2,1,0:T(8,128)(2,1)S(1)} custom-call(bf16[2,4,128,512]{3,2,1,0:T(8,128)(2,1)} %x_hbm.1, bf16[4,3,4608,512]{3,2,1,0:T(8,128)(2,1)} %bitcast.1, f32[4,512]{1,0:T(4,128)} %bias_hbm.1, f32[2,512]{1,0:T(2,128)} %in_scale_hbm.1, f32[2,512]{1,0:T(2,128)} %in_shift_hbm.1, f32[2,2,512]{2,1,0:T(2,128)} %mid_scale_hbm.1, ...), custom_call_target="tpu_custom_call" | custom-call | tf_op jit(solution)/shard_map/pallas_call | solution.py:355
  68.3 1.2 %shard_map.74 = bf16[2,4,128,512]{3,2,1,0:T(8,128)(2,1)} custom-call(bf16[2,4,128,512]{3,2,1,0:T(8,128)(2,1)S(1)} %shard_map.73.val_ref), custom_call_target="tpu_custom_call" | custom-call | tf_op jit(solution)/shard_map/pallas_call | solution.py:400

commit v4 on v3

--- a/solution.py
+++ b/solution.py
@@ -37,25 +37,28 @@
     peers = [lax.rem(cp + d, cp_size) for d in range(1, cp_size)]
     right = lax.rem(cp + 1, cp_size)
 
-    def mm_step(slot, t, k, p, dp, dq, kt):
-        lhs = act[t + k, p + dp, TILE * (1 + dq) : TILE * (1 + dq) + N_COL, kt * HALF : (kt + 1) * HALF]
+    def mm_step(slot, t, k, low, high, dp, dq, kt):
+        cut = slice(TILE * (1 + dq), TILE * (1 + dq) + N_COL)
+        lhs = act[t + k, low + dp : high + dp, cut, kt * HALF : (kt + 1) * HALF].reshape((high - low) * N_COL, HALF)
         off = ((dp + 1) * 3 + dq + 1) * N_CH + kt * HALF
         for m in range(2):
             w = wts[slot, k, off : off + HALF, m * HALF : (m + 1) * HALF]
-            acc[t, p, m] += jnp.dot(lhs, w, preferred_element_type=F32)
+            out = jnp.dot(lhs, w, preferred_element_type=F32)
+            for p in range(low, high):
+                acc[t, p, m] += out[(p - low) * N_COL : (p - low + 1) * N_COL]
 
     def pop(m, t, p):
         val = acc[t, p, m]
         acc[t, p, m] = jnp.zeros((N_COL, HALF), F32)
         return val
 
-    def steps_of(t, k, kts=(0, 1), rows=range(N_ROW), dps=(0, 1, -1)):
+    def steps_of(t, k, kts=(0, 1), rows=(0, N_ROW), dps=(0, 1, -1), size=N_ROW):
         return [
-            (t, k, p, dp, dq, kt)
+            (t, k, max(low, -dp), min(low + size, N_ROW - dp, rows[1]), dp, dq, kt)
             for kt in kts
-            for p in rows
+            for low in range(rows[0], rows[1], size)
             for dp in dps
-            if 0 <= p + dp < N_ROW
+            if max(low, -dp) < min(low + size, N_ROW - dp, rows[1])
             for dq in (0, -1, 1)
         ]
 
@@ -207,10 +210,10 @@
 
                 @pl.when(jnp.logical_not(last))
                 def _():
-                    if piece == 0:
+                    halo_copy(0, 0, piece).start()
+                    if piece == len(PIECES) - 1:
                         for i in range(2):
                             param_copy(i).start()
-                    halo_copy(0, 0, piece).start()
 
     @pl.when(first)
     def _():
@@ -229,7 +232,7 @@
         for d in range(cp_size - 1):
             st_copy(par, d).wait()
         mean, rstd = statistics(par)
-        coefficients(c, mean, rstd, (3, 2))
+        coefficients(c, mean, rstd, (3,))
 
         def own(t):
             return lambda p, cut: raw[par, t, p, :, cut]
@@ -246,7 +249,7 @@
         for thunk in norms(own(1), 3, (0,), (0, 1)):
             thunk()
 
-        @pl.when(c == 0)
+        @pl.when(c == 1)
         def _():
             @pl.when(jnp.logical_not(first))
             def _():
@@ -268,35 +271,35 @@
                 for i in range(2):
                     param_copy(i).wait_send()
 
-        coefficients(c, mean, rstd, (1, 0))
+        coefficients(c, mean, rstd, (2, 1, 0))
         w_copy(c, 2).wait()
         w_copy(c, 1).wait()
-        run(par, steps_of(1, 2, (0,)), norms(own(1), 3, (0,), (2, 3)) + norms(own(1), 3, (1,)), 0.9)
+        run(par, steps_of(1, 2, (0,), size=1), norms(own(1), 3, (0,), (2, 3)) + norms(own(1), 3, (1,)), 0.9)
         run(par, steps_of(1, 2, (1,)), norms(own(0), 2))
         run(par, steps_of(1, 1))
         w_copy(c, 0).wait()
         own_copy(par, par, 0).wait()
         steps = steps_of(0, 2)
-        run(par, steps[:40], norms(received(1), 1, rows=(0, 1)), 0.9)
+        run(par, steps[:12], norms(received(1), 1, rows=(0, 1)), 0.9)
         own_copy(par, par, 1).wait()
-        run(par, steps[40:], norms(received(1), 1, rows=(2, 3)), 0.9)
+        run(par, steps[12:], norms(received(1), 1, rows=(2, 3)), 0.9)
         run(par, steps_of(1, 0, dps=(1, -1)))
         for p in range(N_ROW):
-            run(par, steps_of(1, 0, rows=(p,), dps=(0,)), epilogues(1, (p - 1,)) if p else ())
+            run(par, steps_of(1, 0, rows=(p, p + 1), dps=(0,)), epilogues(1, (p - 1,)) if p else ())
         steps = steps_of(0, 1)
-        run(par, steps[:8], epilogues(1, (3,)))
+        run(par, steps[:3], epilogues(1, (3,)))
 
         @pl.when(jnp.logical_and(c < N_CONV - 1, jnp.logical_not(last)))
         def _():
             halo_copy(nxt, nxt, 0).start()
 
         own_copy(par, par, 2).wait()
-        run(par, steps[8:52], norms(received(0), 0, rows=(0, 1)), 0.9)
+        run(par, steps[3:15], norms(received(0), 0, rows=(0, 1)), 0.9)
         own_copy(par, par, 3).wait()
-        run(par, steps[52:], norms(received(0), 0, rows=(2, 3)), 0.9)
+        run(par, steps[15:], norms(received(0), 0, rows=(2, 3)), 0.9)
         run(par, steps_of(0, 0, dps=(1, -1)))
         for p in range(N_ROW):
-            run(par, steps_of(0, 0, rows=(p,), dps=(0,)), epilogues(0, (p - 1,)) if p else ())
+            run(par, steps_of(0, 0, rows=(p, p + 1), dps=(0,)), epilogues(0, (p - 1,)) if p else ())
         for thunk in epilogues(0, (N_ROW - 1,)):
             thunk()
         finish_moments(nxt)

time: 69.6 us -> 69.4 us (level)
  no operation moved by 1% of the time
where the time goes in v4:
time: 69.4 us; the launch traced here: 69.3 us
  Pallas kernels  69.3 us (100%)
    pallas_call x1, Pallas kernels, local_decode(): pl.pallas_call(functools.partial(kernel, cp_size), out_shape=jax.ShapeDty...  68.1 us

profile of v4, /device:TPU:0, one launch (start us, length us, event | category | flops | bytes accessed | tf_op | source)
XLA Modules:
  0.0 69.3 jit_solution(10558635210994431476)
XLA Ops:
  0.0 68.1 %shard_map.73.val_ref = bf16[2,4,128,512]{3,2,1,0:T(8,128)(2,1)S(1)} custom-call(bf16[2,4,128,512]{3,2,1,0:T(8,128)(2,1)} %x_hbm.1, bf16[4,3,4608,512]{3,2,1,0:T(8,128)(2,1)} %bitcast.1, f32[4,512]{1,0:T(4,128)} %bias_hbm.1, f32[2,512]{1,0:T(2,128)} %in_scale_hbm.1, f32[2,512]{1,0:T(2,128)} %in_shift_hbm.1, f32[2,2,512]{2,1,0:T(2,128)} %mid_scale_hbm.1, ...), custom_call_target="tpu_custom_call" | custom-call | tf_op jit(solution)/shard_map/pallas_call | solution.py:358
  68.1 1.2 %shard_map.74 = bf16[2,4,128,512]{3,2,1,0:T(8,128)(2,1)} custom-call(bf16[2,4,128,512]{3,2,1,0:T(8,128)(2,1)S(1)} %shard_map.73.val_ref), custom_call_target="tpu_custom_call" | custom-call | tf_op jit(solution)/shard_map/pallas_call | solution.py:403

commit v5 on v4

--- a/solution.py
+++ b/solution.py
@@ -108,16 +108,15 @@
         for d in range(cp_size - 1):
             total = total + rx[slot, d]
         lane = lax.broadcasted_iota(jnp.int32, total.shape, 1)
-        for unit in (1, 4):
-            spot = (lane // unit) % 4
-            terms = [total]
-            for d in range(1, 4):
-                up, down = pltpu.roll(total, 128 - d * unit, 1), pltpu.roll(total, d * unit, 1)
-                terms.append(jnp.where(spot < 4 - d, up, 0.0))
-                terms.append(jnp.where(spot >= d, down, 0.0))
-            while len(terms) > 1:
-                terms = [terms[i] + terms[i + 1] for i in range(0, len(terms) - 1, 2)] + terms[len(terms) & ~1 :]
-            total = terms[0]
+        size = N_CH // NUM_GROUPS
+        spot = lane % size
+        terms = [total]
+        for d in range(1, size):
+            terms.append(jnp.where(spot < size - d, pltpu.roll(total, 128 - d, 1), 0.0))
+            terms.append(jnp.where(spot >= d, pltpu.roll(total, d, 1), 0.0))
+        while len(terms) > 1:
+            terms = [terms[i] + terms[i + 1] for i in range(0, len(terms) - 1, 2)] + terms[len(terms) & ~1 :]
+        total = terms[0]
         mean = total[0:4] * (1.0 / count)
         var = total[4:8] * (1.0 / count) - mean * mean
         return mean, lax.rsqrt(var + EPSILON)
@@ -170,7 +169,7 @@
     small_copies = [pltpu.make_async_copy(src, dst, s_sem.at[i]) for i, (src, dst) in enumerate(small)]
     for copy in small_copies:
         copy.start()
-    for k in (2, 1, 0):
+    for k in (2, 1):
         w_copy(0, k).start()
 
     part[...] = jnp.zeros_like(part)
@@ -224,11 +223,6 @@
         par = lax.rem(c, 2)
         nxt = 1 - par
 
-        @pl.when(c < N_CONV - 1)
-        def _():
-            for k in (2, 1, 0):
-                w_copy(c + 1, k).start()
-
         for d in range(cp_size - 1):
             st_copy(par, d).wait()
         mean, rstd = statistics(par)
@@ -248,6 +242,15 @@
 
         for thunk in norms(own(1), 3, (0,), (0, 1)):
             thunk()
+
+        @pl.when(c == 0)
+        def _():
+            w_copy(0, 0).start()
+
+        @pl.when(c < N_CONV - 1)
+        def _():
+            for k in (2, 1, 0):
+                w_copy(c + 1, k).start()
 
         @pl.when(c == 1)
         def _():
@@ -277,12 +280,12 @@
         run(par, steps_of(1, 2, (0,), size=1), norms(own(1), 3, (0,), (2, 3)) + norms(own(1), 3, (1,)), 0.9)
         run(par, steps_of(1, 2, (1,)), norms(own(0), 2))
         run(par, steps_of(1, 1))
+        steps = steps_of(0, 2)
+        run(par, steps[:12])
         w_copy(c, 0).wait()
         own_copy(par, par, 0).wait()
-        steps = steps_of(0, 2)
-        run(par, steps[:12], norms(received(1), 1, rows=(0, 1)), 0.9)
         own_copy(par, par, 1).wait()
-        run(par, steps[12:], norms(received(1), 1, rows=(2, 3)), 0.9)
+        run(par, steps[12:], norms(received(1), 1), 0.9)
         run(par, steps_of(1, 0, dps=(1, -1)))
         for p in range(N_ROW):
             run(par, steps_of(1, 0, rows=(p, p + 1), dps=(0,)), epilogues(1, (p - 1,)) if p else ())

time: 69.4 us -> 67.8 us (0.977)
  Pallas kernels: 69.3 us -> 67.7 us
    pallas_call x1, Pallas kernels: 68.1 us -> 66.5 us  [local_decode(): pl.pallas_call(functools.partial(kernel, cp_size), out_shape=jax.ShapeDty...]
where the time goes in v5:
time: 67.8 us; the launch traced here: 67.7 us
  Pallas kernels  67.7 us (100%)
    pallas_call x1, Pallas kernels, local_decode(): pl.pallas_call(functools.partial(kernel, cp_size), out_shape=jax.ShapeDty...  66.5 us

profile of v5, /device:TPU:0, one launch (start us, length us, event | category | flops | bytes accessed | tf_op | source)
XLA Modules:
  0.0 67.7 jit_solution(8518207360494788943)
XLA Ops:
  0.0 66.5 %shard_map.73.val_ref = bf16[2,4,128,512]{3,2,1,0:T(8,128)(2,1)S(1)} custom-call(bf16[2,4,128,512]{3,2,1,0:T(8,128)(2,1)} %x_hbm.1, bf16[4,3,4608,512]{3,2,1,0:T(8,128)(2,1)} %bitcast.1, f32[4,512]{1,0:T(4,128)} %bias_hbm.1, f32[2,512]{1,0:T(2,128)} %in_scale_hbm.1, f32[2,512]{1,0:T(2,128)} %in_shift_hbm.1, f32[2,2,512]{2,1,0:T(2,128)} %mid_scale_hbm.1, ...), custom_call_target="tpu_custom_call" | custom-call | tf_op jit(solution)/shard_map/pallas_call | solution.py:361
  66.5 1.2 %shard_map.74 = bf16[2,4,128,512]{3,2,1,0:T(8,128)(2,1)} custom-call(bf16[2,4,128,512]{3,2,1,0:T(8,128)(2,1)S(1)} %shard_map.73.val_ref), custom_call_target="tpu_custom_call" | custom-call | tf_op jit(solution)/shard_map/pallas_call | solution.py:406

commit v6 on v5

--- a/solution.py
+++ b/solution.py
@@ -169,8 +169,6 @@
     small_copies = [pltpu.make_async_copy(src, dst, s_sem.at[i]) for i, (src, dst) in enumerate(small)]
     for copy in small_copies:
         copy.start()
-    for k in (2, 1):
-        w_copy(0, k).start()
 
     part[...] = jnp.zeros_like(part)
     acc[...] = jnp.zeros_like(acc)
@@ -185,6 +183,7 @@
     pl.semaphore_wait(barrier, cp_size - 1)
     for d in range(cp_size - 1):
         st_copy(0, d).start()
+    w_copy(0, 2).start()
 
     for copy in small_copies:
         copy.wait()
@@ -245,7 +244,8 @@
 
         @pl.when(c == 0)
         def _():
-            w_copy(0, 0).start()
+            for k in (1, 0):
+                w_copy(0, k).start()
 
         @pl.when(c < N_CONV - 1)
         def _():
@@ -276,9 +276,9 @@
 
         coefficients(c, mean, rstd, (2, 1, 0))
         w_copy(c, 2).wait()
-        w_copy(c, 1).wait()
         run(par, steps_of(1, 2, (0,), size=1), norms(own(1), 3, (0,), (2, 3)) + norms(own(1), 3, (1,)), 0.9)
         run(par, steps_of(1, 2, (1,)), norms(own(0), 2))
+        w_copy(c, 1).wait()
         run(par, steps_of(1, 1))
         steps = steps_of(0, 2)
         run(par, steps[:12])

time: 67.8 us -> 67.9 us (level)
  no operation moved by 1% of the time
where the time goes in v6:
time: 67.9 us; the launch traced here: 67.8 us
  Pallas kernels  67.7 us (100%)
    pallas_call x1, Pallas kernels, local_decode(): pl.pallas_call(functools.partial(kernel, cp_size), out_shape=jax.ShapeDty...  66.6 us

profile of v6, /device:TPU:0, one launch (start us, length us, event | category | flops | bytes accessed | tf_op | source)
XLA Modules:
  0.0 67.8 jit_solution(14184724859053774614)
XLA Ops:
  0.0 66.6 %shard_map.73.val_ref = bf16[2,4,128,512]{3,2,1,0:T(8,128)(2,1)S(1)} custom-call(bf16[2,4,128,512]{3,2,1,0:T(8,128)(2,1)} %x_hbm.1, bf16[4,3,4608,512]{3,2,1,0:T(8,128)(2,1)} %bitcast.1, f32[4,512]{1,0:T(4,128)} %bias_hbm.1, f32[2,512]{1,0:T(2,128)} %in_scale_hbm.1, f32[2,512]{1,0:T(2,128)} %in_shift_hbm.1, f32[2,2,512]{2,1,0:T(2,128)} %mid_scale_hbm.1, ...), custom_call_target="tpu_custom_call" | custom-call | tf_op jit(solution)/shard_map/pallas_call | solution.py:361
  66.6 1.2 %shard_map.74 = bf16[2,4,128,512]{3,2,1,0:T(8,128)(2,1)} custom-call(bf16[2,4,128,512]{3,2,1,0:T(8,128)(2,1)S(1)} %shard_map.73.val_ref), custom_call_target="tpu_custom_call" | custom-call | tf_op jit(solution)/shard_map/pallas_call | solution.py:406

commit v7 on v6

--- a/solution.py
+++ b/solution.py
@@ -247,11 +247,6 @@
             for k in (1, 0):
                 w_copy(0, k).start()
 
-        @pl.when(c < N_CONV - 1)
-        def _():
-            for k in (2, 1, 0):
-                w_copy(c + 1, k).start()
-
         @pl.when(c == 1)
         def _():
             @pl.when(jnp.logical_not(first))
@@ -279,6 +274,12 @@
         run(par, steps_of(1, 2, (0,), size=1), norms(own(1), 3, (0,), (2, 3)) + norms(own(1), 3, (1,)), 0.9)
         run(par, steps_of(1, 2, (1,)), norms(own(0), 2))
         w_copy(c, 1).wait()
+
+        @pl.when(c < N_CONV - 1)
+        def _():
+            for k in (2, 1, 0):
+                w_copy(c + 1, k).start()
+
         run(par, steps_of(1, 1))
         steps = steps_of(0, 2)
         run(par, steps[:12])

time: 67.9 us -> 67.9 us (level)
  no operation moved by 1% of the time
where the time goes in v7:
time: 67.9 us; the launch traced here: 67.8 us
  Pallas kernels  67.8 us (100%)
    pallas_call x1, Pallas kernels, local_decode(): pl.pallas_call(functools.partial(kernel, cp_size), out_shape=jax.ShapeDty...  66.6 us

profile of v7, /device:TPU:0, one launch (start us, length us, event | category | flops | bytes accessed | tf_op | source)
XLA Modules:
  0.0 67.8 jit_solution(10554950253871550659)
XLA Ops:
  0.0 66.6 %shard_map.73.val_ref = bf16[2,4,128,512]{3,2,1,0:T(8,128)(2,1)S(1)} custom-call(bf16[2,4,128,512]{3,2,1,0:T(8,128)(2,1)} %x_hbm.1, bf16[4,3,4608,512]{3,2,1,0:T(8,128)(2,1)} %bitcast.1, f32[4,512]{1,0:T(4,128)} %bias_hbm.1, f32[2,512]{1,0:T(2,128)} %in_scale_hbm.1, f32[2,512]{1,0:T(2,128)} %in_shift_hbm.1, f32[2,2,512]{2,1,0:T(2,128)} %mid_scale_hbm.1, ...), custom_call_target="tpu_custom_call" | custom-call | tf_op jit(solution)/shard_map/pallas_call | solution.py:362
  66.6 1.2 %shard_map.74 = bf16[2,4,128,512]{3,2,1,0:T(8,128)(2,1)} custom-call(bf16[2,4,128,512]{3,2,1,0:T(8,128)(2,1)S(1)} %shard_map.73.val_ref), custom_call_target="tpu_custom_call" | custom-call | tf_op jit(solution)/shard_map/pallas_call | solution.py:407

commit v8 on v7

--- a/solution.py
+++ b/solution.py
@@ -169,6 +169,7 @@
     small_copies = [pltpu.make_async_copy(src, dst, s_sem.at[i]) for i, (src, dst) in enumerate(small)]
     for copy in small_copies:
         copy.start()
+    w_copy(0, 2).start()
 
     part[...] = jnp.zeros_like(part)
     acc[...] = jnp.zeros_like(acc)
@@ -183,7 +184,6 @@
     pl.semaphore_wait(barrier, cp_size - 1)
     for d in range(cp_size - 1):
         st_copy(0, d).start()
-    w_copy(0, 2).start()
 
     for copy in small_copies:
         copy.wait()

time: 67.9 us -> 67.9 us (level)
  no operation moved by 1% of the time
where the time goes in v8:
time: 67.9 us; the launch traced here: 67.8 us
  Pallas kernels  67.8 us (100%)
    pallas_call x1, Pallas kernels, local_decode(): pl.pallas_call(functools.partial(kernel, cp_size), out_shape=jax.ShapeDty...  66.6 us

profile of v8, /device:TPU:0, one launch (start us, length us, event | category | flops | bytes accessed | tf_op | source)
XLA Modules:
  0.0 67.8 jit_solution(5369493751852067336)
XLA Ops:
  0.0 66.6 %shard_map.73.val_ref = bf16[2,4,128,512]{3,2,1,0:T(8,128)(2,1)S(1)} custom-call(bf16[2,4,128,512]{3,2,1,0:T(8,128)(2,1)} %x_hbm.1, bf16[4,3,4608,512]{3,2,1,0:T(8,128)(2,1)} %bitcast.1, f32[4,512]{1,0:T(4,128)} %bias_hbm.1, f32[2,512]{1,0:T(2,128)} %in_scale_hbm.1, f32[2,512]{1,0:T(2,128)} %in_shift_hbm.1, f32[2,2,512]{2,1,0:T(2,128)} %mid_scale_hbm.1, ...), custom_call_target="tpu_custom_call" | custom-call | tf_op jit(solution)/shard_map/pallas_call | solution.py:362
  66.6 1.2 %shard_map.74 = bf16[2,4,128,512]{3,2,1,0:T(8,128)(2,1)} custom-call(bf16[2,4,128,512]{3,2,1,0:T(8,128)(2,1)S(1)} %shard_map.73.val_ref), custom_call_target="tpu_custom_call" | custom-call | tf_op jit(solution)/shard_map/pallas_call | solution.py:407

commit v9 on v5

--- a/solution.py
+++ b/solution.py
@@ -247,11 +247,6 @@
         def _():
             w_copy(0, 0).start()
 
-        @pl.when(c < N_CONV - 1)
-        def _():
-            for k in (2, 1, 0):
-                w_copy(c + 1, k).start()
-
         @pl.when(c == 1)
         def _():
             @pl.when(jnp.logical_not(first))
@@ -285,6 +280,12 @@
         w_copy(c, 0).wait()
         own_copy(par, par, 0).wait()
         own_copy(par, par, 1).wait()
+
+        @pl.when(c < N_CONV - 1)
+        def _():
+            for k in (2, 1, 0):
+                w_copy(c + 1, k).start()
+
         run(par, steps[12:], norms(received(1), 1), 0.9)
         run(par, steps_of(1, 0, dps=(1, -1)))
         for p in range(N_ROW):

time: 67.8 us -> 67.8 us (level)
  no operation moved by 1% of the time
where the time goes in v9:
time: 67.8 us; the launch traced here: 67.7 us
  Pallas kernels  67.7 us (100%)
    pallas_call x1, Pallas kernels, local_decode(): pl.pallas_call(functools.partial(kernel, cp_size), out_shape=jax.ShapeDty...  66.5 us

profile of v9, /device:TPU:0, one launch (start us, length us, event | category | flops | bytes accessed | tf_op | source)
XLA Modules:
  0.0 67.7 jit_solution(5036724109896413254)
XLA Ops:
  0.0 66.5 %shard_map.73.val_ref = bf16[2,4,128,512]{3,2,1,0:T(8,128)(2,1)S(1)} custom-call(bf16[2,4,128,512]{3,2,1,0:T(8,128)(2,1)} %x_hbm.1, bf16[4,3,4608,512]{3,2,1,0:T(8,128)(2,1)} %bitcast.1, f32[4,512]{1,0:T(4,128)} %bias_hbm.1, f32[2,512]{1,0:T(2,128)} %in_scale_hbm.1, f32[2,512]{1,0:T(2,128)} %in_shift_hbm.1, f32[2,2,512]{2,1,0:T(2,128)} %mid_scale_hbm.1, ...), custom_call_target="tpu_custom_call" | custom-call | tf_op jit(solution)/shard_map/pallas_call | solution.py:362
  66.5 1.2 %shard_map.74 = bf16[2,4,128,512]{3,2,1,0:T(8,128)(2,1)} custom-call(bf16[2,4,128,512]{3,2,1,0:T(8,128)(2,1)S(1)} %shard_map.73.val_ref), custom_call_target="tpu_custom_call" | custom-call | tf_op jit(solution)/shard_map/pallas_call | solution.py:407

commit v10 on v5

--- a/solution.py
+++ b/solution.py
@@ -94,6 +94,7 @@
         conv = (pop(m, t, p) + bias_ref[pl.ds(c, 1), cut]).astype(BF16).astype(F32)
         val = (raw[2 - 2 * par, t, p, :, cut].astype(F32) + conv).astype(BF16)
         raw[1 - par, t, p, :, cut] = val
+        out_ref[t, p, :, cut] = val
         add_moments(val.astype(F32), m)
 
     def finish_moments(slot):
@@ -330,8 +331,6 @@
         return carry
 
     lax.fori_loop(0, N_CONV, conv, 0)
-
-    out_ref[...] = raw[0]
 
 
 def reorder(val_ref, out_hbm, tmp, buf, sem):

time: 67.8 us -> 67.8 us (level)
  no operation moved by 1% of the time
where the time goes in v10:
time: 67.8 us; the launch traced here: 67.7 us
  Pallas kernels  67.7 us (100%)
    pallas_call x1, Pallas kernels, local_decode(): pl.pallas_call(functools.partial(kernel, cp_size), out_shape=jax.ShapeDty...  66.5 us

profile of v10, /device:TPU:0, one launch (start us, length us, event | category | flops | bytes accessed | tf_op | source)
XLA Modules:
  0.0 67.7 jit_solution(7344400468585431773)
XLA Ops:
  0.0 66.5 %shard_map.73.val_ref = bf16[2,4,128,512]{3,2,1,0:T(8,128)(2,1)S(1)} custom-call(bf16[2,4,128,512]{3,2,1,0:T(8,128)(2,1)} %x_hbm.1, bf16[4,3,4608,512]{3,2,1,0:T(8,128)(2,1)} %bitcast.1, f32[4,512]{1,0:T(4,128)} %bias_hbm.1, f32[2,512]{1,0:T(2,128)} %in_scale_hbm.1, f32[2,512]{1,0:T(2,128)} %in_shift_hbm.1, f32[2,2,512]{2,1,0:T(2,128)} %mid_scale_hbm.1, ...), custom_call_target="tpu_custom_call" | custom-call | tf_op jit(solution)/shard_map/pallas_call | solution.py:360
  66.5 1.2 %shard_map.74 = bf16[2,4,128,512]{3,2,1,0:T(8,128)(2,1)} custom-call(bf16[2,4,128,512]{3,2,1,0:T(8,128)(2,1)S(1)} %shard_map.73.val_ref), custom_call_target="tpu_custom_call" | custom-call | tf_op jit(solution)/shard_map/pallas_call | solution.py:405
